TPU v7x, 32 devices: a whole 2x2x4 slice. The times are simulated.
32 devices in a mesh: gx: 4 (over z), gy: 2 (over x), gz: 4 (over y, core).
Axes of the slice: x: 2, y: 2, z: 4, core: 2. Of those that a mesh axis runs over, the one named last changes fastest.
Arguments:
- fields: bfloat16 [5, 128, 96, 512], P(None, 'gx', 'gy', 'gz'), may hold values from -8 to 8
Outputs:
- filtered: bfloat16 [5, 128, 96, 512], P(None, 'gx', 'gy', 'gz')
- stress: bfloat16 [15, 128, 96, 512], P(None, 'gx', 'gy', 'gz')
All inputs are finite; a program needn't handle non-finite values.
Results may differ from a plain program's by a relative error of at most 0.0022.
Values may be sent and summed in bfloat16 or wider, within the bound.
A program may use at most 128 MiB of HBM per device.

v0:
```python
import functools

import jax
import jax.numpy as jnp
from jax import lax
from jax.experimental import pallas as pl
from jax.experimental.pallas import tpu as pltpu
from jax.sharding import PartitionSpec as P

R = 32


pair_first = (0, 0, 0, 0, 0, 1, 1, 1, 1, 2, 2, 2, 3, 3, 4)
pair_second = (0, 1, 2, 3, 4, 1, 2, 3, 4, 2, 3, 4, 3, 4, 4)


def padded(block, sides, width, periodic):
    for axis, dim in sides:
        count = lax.axis_size(axis)
        forward = [(i, i + 1) for i in range(count - 1)]
        if periodic:
            forward.append((count - 1, 0))
        backward = [(target, source) for source, target in forward]
        low = lax.ppermute(
            lax.slice_in_dim(block, block.shape[dim] - width, None, axis=dim), axis, forward
        )
        high = lax.ppermute(lax.slice_in_dim(block, 0, width, axis=dim), axis, backward)
        block = jnp.concatenate([low, block, high], axis=dim)
    return block


def taps(offset):
    return jnp.where(jnp.abs(offset) <= R, 1.0, 0.0).astype(jnp.bfloat16)


def banded(count):
    rows = lax.broadcasted_iota(jnp.int32, (count, count + 2 * R), 0)
    cols = lax.broadcasted_iota(jnp.int32, (count, count + 2 * R), 1)
    return taps(cols - rows - R)


def tap_total():
    offsets = jnp.arange(-R, R + 1, dtype=jnp.int32)
    return jnp.sum(taps(offsets).astype(jnp.float32))


def edge_norm(start, count, whole):
    cells = start + jnp.arange(count, dtype=jnp.int32)[:, None]
    offsets = jnp.arange(-R, R + 1, dtype=jnp.int32)[None, :]
    inside = (cells + offsets >= 0) & (cells + offsets < whole)
    return jnp.sum(jnp.where(inside, taps(offsets).astype(jnp.float32), 0.0), axis=1)


def streamwise_section(block, across, norm_x):
    plain = (
        jnp.einsum("im,cmyz->ciyz", across, block, preferred_element_type=jnp.float32) / norm_x
    ).astype(jnp.bfloat16)
    first_table = jnp.array(pair_first, jnp.int32)
    second_table = jnp.array(pair_second, jnp.int32)

    def product_filter(pair):
        left = lax.dynamic_index_in_dim(block, first_table[pair], 0, keepdims=False)
        right = lax.dynamic_index_in_dim(block, second_table[pair], 0, keepdims=False)
        product = (left.astype(jnp.float32) * right.astype(jnp.float32)).astype(jnp.bfloat16)
        result = jnp.einsum("im,myz->iyz", across, product, preferred_element_type=jnp.float32)
        return (result / norm_x).astype(jnp.bfloat16)

    products = lax.map(product_filter, jnp.arange(15, dtype=jnp.int32))
    return jnp.concatenate([plain, products], 0)


def finish(smooth):
    filtered = smooth[:5]
    stress = jnp.stack(
        [
            smooth[5 + pair] - smooth[pair_first[pair]] * smooth[pair_second[pair]]
            for pair in range(15)
        ],
        0,
    )
    return (filtered.astype(jnp.bfloat16), stress.astype(jnp.bfloat16))


def body(fields):
    depth_x = fields.shape[1]
    rimmed = padded(fields, (("gx", 1),), R, False)
    across = banded(depth_x)
    norm_x = edge_norm(lax.axis_index("gx") * depth_x, depth_x, depth_x * lax.axis_size("gx"))[
        :, None, None
    ]
    total = tap_total()
    widened = padded(rimmed, (("gz", 3),), R, True)
    zrimmed = streamwise_section(widened, across, norm_x)
    along_z = banded(fields.shape[3])
    zdone = (
        jnp.einsum("axyk,zk->axyz", zrimmed, along_z, preferred_element_type=jnp.float32) / total
    ).astype(jnp.bfloat16)
    yrimmed = padded(zdone, (("gy", 2),), R, True)
    along_y = banded(zdone.shape[2])
    smooth = (
        jnp.einsum("yj,axjz->axyz", along_y, yrimmed, preferred_element_type=jnp.float32) / total
    )
    filtered, stress = finish(smooth)
    return (filtered, stress)


def filter_kernel(dims, first_table, second_table, scale_x_ref, wz_ref, wy_ref, *refs):
    depth_x, half, depth_z = dims
    sources = refs[:30]
    filtered_ref, stress_ref, center, rims, narrow, means, sems = refs[30:]
    step = pl.program_id(0)
    rows = 2 * half
    inverse = 1.0 / (2 * R + 1)

    def copies(field):
        parts = sources[6 * field : 6 * field + 6]
        places = ((R, depth_x), (0, R), (R + depth_x, R))
        return [
            pltpu.make_async_copy(
                parts[k], held.at[field, pl.ds(*places[k % 3])], sems.at[field, k]
            )
            for k, held in enumerate((center,) * 3 + (rims,) * 3)
        ]

    @pl.when(step == 0)
    def _():
        for field in range(5):
            for copy in copies(field):
                copy.start()

    for field in range(5):

        @pl.when(step == field)
        def _(field=field):
            for copy in copies(field):
                copy.wait()

    left = first_table[step]
    right = second_table[step]

    def streamwise(source, count, column, plain):
        def chunk(index, carry):
            part = pl.ds(pl.multiple_of(index * 16, 16), 16)

            def value(row):
                one = source[left, row, part, :]
                if not plain:
                    one = one * source[right, row, part, :]
                return one.astype(jnp.float32)

            sums = [value(k) for k in range(4)]
            for row in range(4, 2 * R + 1):
                sums[row % 4] = sums[row % 4] + value(row)
            total = (sums[0] + sums[1]) + (sums[2] + sums[3])
            for cell in range(depth_x):
                if cell:
                    total = total + (value(cell + 2 * R) - value(cell - 1))
                narrow[cell, part, pl.ds(column, 128)] = (
                    total * scale_x_ref[cell]
                ).astype(jnp.bfloat16)
            return carry

        lax.fori_loop(0, count // 16, chunk, 0)

    def both(plain):
        streamwise(center, rows, 0, plain)
        streamwise(rims, half, depth_z, plain)

    pl.when(step < 5)(lambda: both(True))
    pl.when(step >= 5)(lambda: both(False))

    def smooth(cell):
        rim = narrow[cell, pl.ds(0, half), pl.ds(depth_z, 128)]
        parts = []
        for side in range(2):
            mid = narrow[cell, pl.ds(side * half, half), pl.ds(0, depth_z)]
            parts.append(
                jnp.dot(
                    jnp.concatenate([mid, rim], 1),
                    wz_ref[side],
                    preferred_element_type=jnp.float32,
                )
            )
        return (jnp.concatenate(parts, 0) * inverse).astype(jnp.bfloat16)

    def pairs(index, carry):
        for sub in range(2):
            cell = 4 * index + 2 * sub
            wide = jnp.concatenate([smooth(cell), smooth(cell + 1)], 1)
            out = jnp.dot(wy_ref[...], wide, preferred_element_type=jnp.float32) * inverse
            for k in range(2):
                g = out[:, k * depth_z : (k + 1) * depth_z]

                @pl.when(step < 5)
                def _(k=k, g=g):
                    means[step, cell + k] = g
                    filtered_ref[0, cell + k] = g.astype(jnp.bfloat16)

                @pl.when(step >= 5)
                def _(k=k, g=g):
                    stress_ref[0, cell + k] = (
                        g - means[left, cell + k] * means[right, cell + k]
                    ).astype(jnp.bfloat16)

        return carry

    lax.fori_loop(0, depth_x // 4, pairs, 0)


def shift(block, axis, by, periodic):
    count = lax.axis_size(axis)
    hops = [(i, (i + by) % count) for i in range(count) if periodic or 0 <= i + by < count]
    return lax.ppermute(block, axis, hops)


def compact(fields):
    _, depth_x, half, depth_z = fields.shape
    quarter = half // 2
    operands = []
    for field in range(5):
        mine = fields[field]
        own = jnp.concatenate([mine, shift(mine, "gy", 1, True)], 1)
        low = shift(own[depth_x - R :], "gx", 1, False)
        high = shift(own[:R], "gx", -1, False)

        def packed(columns):
            edge = own[:, :, columns]
            return jnp.concatenate(
                [edge[:, k * quarter : (k + 1) * quarter] for k in range(4)], 2
            )

        def unpacked(block):
            quarters = [block[:, :, k * R : (k + 1) * R] for k in range(4)]
            return [
                jnp.concatenate(quarters[:2], 1),
                jnp.concatenate(quarters[2:], 1),
            ]

        before = shift(packed(slice(depth_z - R, depth_z)), "gz", 1, True)
        after = shift(packed(slice(0, R)), "gz", -1, True)
        rim = jnp.concatenate(unpacked(before) + unpacked(after), 2)
        rim_low = shift(rim[depth_x - R :], "gx", 1, False)
        rim_high = shift(rim[:R], "gx", -1, False)
        operands += [own, low, high, rim, rim_low, rim_high]

    norm = edge_norm(lax.axis_index("gx") * depth_x, depth_x, depth_x * lax.axis_size("gx"))
    band = banded(depth_z).T
    blank = jnp.zeros((R, depth_z), jnp.bfloat16)
    lower, middle, upper = band[:R], band[R : R + depth_z], band[R + depth_z :]
    along_z = jnp.stack(
        [
            jnp.concatenate([middle, lower, blank, upper, blank], 0),
            jnp.concatenate([middle, blank, lower, blank, upper], 0),
        ]
    )
    rows = 2 * half
    gap = jnp.arange(rows)[None, :] - jnp.arange(half)[:, None]
    gap = (gap + half) % rows - half
    along_y = taps(gap)
    first_table = jnp.array(tuple(range(5)) + pair_first, jnp.int32)
    second_table = jnp.array(tuple(range(5)) + pair_second, jnp.int32)
    block = (1, depth_x, half, depth_z)
    smem = pl.BlockSpec(memory_space=pltpu.SMEM)
    vmem = pl.BlockSpec(memory_space=pltpu.VMEM)
    return pl.pallas_call(
        functools.partial(filter_kernel, (depth_x, half, depth_z)),
        grid=(20,),
        in_specs=[smem, smem, smem, vmem, vmem] + [pl.BlockSpec(memory_space=pl.ANY)] * 30,
        out_specs=[
            pl.BlockSpec(block, lambda c: (jnp.minimum(c, 4), 0, 0, 0)),
            pl.BlockSpec(block, lambda c: (jnp.maximum(c - 5, 0), 0, 0, 0)),
        ],
        out_shape=[
            jax.ShapeDtypeStruct((5,) + block[1:], jnp.bfloat16),
            jax.ShapeDtypeStruct((15,) + block[1:], jnp.bfloat16),
        ],
        scratch_shapes=[
            pltpu.VMEM((5, depth_x + 2 * R, rows, depth_z), jnp.bfloat16),
            pltpu.VMEM((5, depth_x + 2 * R, half, 4 * R), jnp.bfloat16),
            pltpu.VMEM((depth_x, rows, depth_z + 4 * R), jnp.bfloat16),
            pltpu.VMEM((5, depth_x, half, depth_z), jnp.float32),
            pltpu.SemaphoreType.DMA((5, 6)),
        ],
        compiler_params=pltpu.CompilerParams(vmem_limit_bytes=56 * 1024 * 1024),
    )(first_table, second_table, 1.0 / norm, along_z, along_y, *operands)


def solution(mesh):
    in_specs = (P(None, "gx", "gy", "gz"),)
    out_specs = (P(None, "gx", "gy", "gz"), P(None, "gx", "gy", "gz"))

    def local(fields):
        _, depth_x, half, depth_z = fields.shape
        fits = (
            mesh.shape["gy"] == 2
            and half % 16 == 0
            and 2 * half >= 2 * R + 1
            and depth_x >= R
            and depth_x % 4 == 0
            and depth_z == 4 * R
        )
        return tuple(compact(fields)) if fits else body(fields)

    return jax.shard_map(local, mesh=mesh, in_specs=in_specs, out_specs=out_specs, check_vma=False)
```

profile of v0, /device:TPU:1, one launch (start us, length us, event | category | flops | bytes accessed | tf_op | source)
XLA Modules:
  0.0 328.6 jit_solution(14899187381250537076)
XLA Ops:
  13.0 25.7 %collective-permute-done = bf16[32,48,128]{2,1,0:T(8,128)(2,1)S(1)} collective-permute-done((bf16[32,48,128]{2,1,0:T(8,128)(2,1)S(1)}, bf16[32,48,128]{2,1,0:T(8,128)(2,1)S(1)}, u32[]{:S(2)}, u32[]{:S(2)}) %collective-permute-start) | collective-permute-done | bytes 393248 | tf_op jit(solution)/shard_map/ppermute | solution.py:213
  39.1 3.8 %collective-permute-start.3 = (bf16[32,24,128]{2,1,0:T(8,128)(2,1)S(1)}, bf16[32,24,128]{2,1,0:T(8,128)(2,1)S(1)}, u32[]{:S(2)}, u32[]{:S(2)}) collective-permute-start(bf16[32,24,128]{2,1,0:T(8,128)(2,1)S(1)} %pad_maximum_fusion.5), channel_id=1, source_target_pairs={{0,1},{1,2},{2,3},{3,0},{4,5},{5,6},{6,7},{7,4},{8,9},{9,10},{10,1... | collective-permute-start | bytes 589832 | tf_op jit(solution)/shard_map/ppermute | solution.py:213
  44.3 2.8 collective-permute-done.21
  55.3 4.1 %collective-permute-done.25 = bf16[32,24,128]{2,1,0:T(8,128)(2,1)S(1)} collective-permute-done((bf16[32,24,128]{2,1,0:T(8,128)(2,1)S(1)}, bf16[32,24,128]{2,1,0:T(8,128)(2,1)S(1)}, u32[]{:S(2)}, u32[]{:S(2)}) %collective-permute-start.25) | collective-permute-done | bytes 196640 | tf_op jit(solution)/shard_map/ppermute | solution.py:213
  63.5 4.6 %collective-permute-done.11 = bf16[32,24,128]{2,1,0:T(8,128)(2,1)S(1)} collective-permute-done((bf16[32,24,128]{2,1,0:T(8,128)(2,1)S(1)}, bf16[32,24,128]{2,1,0:T(8,128)(2,1)S(1)}, u32[]{:S(2)}, u32[]{:S(2)}) %collective-permute-start.11) | collective-permute-done | bytes 196640 | tf_op jit(solution)/shard_map/ppermute | solution.py:213
  68.1 3.2 collective-permute-start.5
  73.1 4.0 %collective-permute-start.26 = (bf16[32,48,128]{2,1,0:T(8,128)(2,1)S(1)}, bf16[32,48,128]{2,1,0:T(8,128)(2,1)S(1)}, u32[]{:S(2)}, u32[]{:S(2)}) collective-permute-start(bf16[32,48,128]{2,1,0:T(8,128)(2,1)S(1)} %maximum_maximum_fusion.3.refs_21_), channel_id=1, source_target_pairs={{0,8},{8,16},{16,24},{1,9},{9,17},{17,25},{2,10},{10,18},{18,26},{... | collective-permute-start | bytes 1179656 | tf_op jit(solution)/shard_map/ppermute | solution.py:213
  80.1 4.0 %collective-permute-start.33 = (bf16[32,48,128]{2,1,0:T(8,128)(2,1)S(1)}, bf16[32,48,128]{2,1,0:T(8,128)(2,1)S(1)}, u32[]{:S(2)}, u32[]{:S(2)}) collective-permute-start(bf16[32,48,128]{2,1,0:T(8,128)(2,1)S(1)} %maximum_maximum_fusion.4.refs_27_), channel_id=1, source_target_pairs={{0,8},{8,16},{16,24},{1,9},{9,17},{17,25},{2,10},{10,18},{18,26},{... | collective-permute-start | bytes 1179656 | tf_op jit(solution)/shard_map/ppermute | solution.py:213
  85.5 4.0 %collective-permute-start.12 = (bf16[32,48,128]{2,1,0:T(8,128)(2,1)S(1)}, bf16[32,48,128]{2,1,0:T(8,128)(2,1)S(1)}, u32[]{:S(2)}, u32[]{:S(2)}) collective-permute-start(bf16[32,48,128]{2,1,0:T(8,128)(2,1)S(1)} %maximum_maximum_fusion.1.refs_9_), channel_id=1, source_target_pairs={{0,8},{8,16},{16,24},{1,9},{9,17},{17,25},{2,10},{10,18},{18,26},{... | collective-permute-start | bytes 1179656 | tf_op jit(solution)/shard_map/ppermute | solution.py:213
  93.0 3.9 %collective-permute-start.19 = (bf16[32,48,128]{2,1,0:T(8,128)(2,1)S(1)}, bf16[32,48,128]{2,1,0:T(8,128)(2,1)}, u32[]{:S(2)}, u32[]{:S(2)}) collective-permute-start(bf16[32,48,128]{2,1,0:T(8,128)(2,1)S(1)} %maximum_maximum_fusion.2.refs_15_), channel_id=1, source_target_pairs={{0,8},{8,16},{16,24},{1,9},{9,17},{17,25},{2,10},{10,18},{18,26},{... | collective-permute-start | bytes 1179656 | tf_op jit(solution)/shard_map/ppermute | solution.py:213
  101.4 3.2 collective-permute-start.29
  106.8 3.1 collective-permute-done.20.refs_17_
  109.9 3.3 %collective-permute-start.15 = (bf16[32,96,128]{2,1,0:T(8,128)(2,1)S(1)}, bf16[32,96,128]{2,1,0:T(8,128)(2,1)S(1)}, u32[]{:S(2)}, u32[]{:S(2)}) collective-permute-start(bf16[32,96,128]{2,1,0:T(8,128)(2,1)S(1)} %pad_maximum_fusion.2.refs_12_), channel_id=1, source_target_pairs={{0,8},{8,16},{16,24},{1,9},{9,17},{17,25},{2,10},{10,18},{18,26},{... | collective-permute-start | bytes 2359304 | tf_op jit(solution)/shard_map/ppermute | solution.py:213
  116.8 9.9 %collective-permute-done.30.refs_26_ = bf16[32,96,128]{2,1,0:T(8,128)(2,1)S(1)} collective-permute-done((bf16[32,96,128]{2,1,0:T(8,128)(2,1)S(1)}, bf16[32,96,128]{2,1,0:T(8,128)(2,1)S(1)}, u32[]{:S(2)}, u32[]{:S(2)}) %collective-permute-start.30) | collective-permute-done | bytes 786464 | tf_op jit(solution)/shard_map/ppermute | solution.py:213
  126.7 3.2 collective-permute-start.8
  132.0 11.5 %collective-permute-done.16.refs_14_ = bf16[32,96,128]{2,1,0:T(8,128)(2,1)S(1)} collective-permute-done((bf16[32,96,128]{2,1,0:T(8,128)(2,1)S(1)}, bf16[32,96,128]{2,1,0:T(8,128)(2,1)S(1)}, u32[]{:S(2)}, u32[]{:S(2)}) %collective-permute-start.16) | collective-permute-done | bytes 786464 | tf_op jit(solution)/shard_map/ppermute | solution.py:213
  143.6 3.2 collective-permute-start.1
  148.9 11.5 %collective-permute-done.9.refs_8_ = bf16[32,96,128]{2,1,0:T(8,128)(2,1)S(1)} collective-permute-done((bf16[32,96,128]{2,1,0:T(8,128)(2,1)S(1)}, bf16[32,96,128]{2,1,0:T(8,128)(2,1)S(1)}, u32[]{:S(2)}, u32[]{:S(2)}) %collective-permute-start.9) | collective-permute-done | bytes 786464 | tf_op jit(solution)/shard_map/ppermute | solution.py:213
  160.4 4.1 %collective-permute-start.22 = (bf16[32,96,128]{2,1,0:T(8,128)(2,1)S(1)}, bf16[32,96,128]{2,1,0:T(8,128)(2,1)}, u32[]{:S(2)}, u32[]{:S(2)}) collective-permute-start(bf16[32,96,128]{2,1,0:T(8,128)(2,1)S(1)} %pad_maximum_fusion.3.refs_18_), channel_id=1, source_target_pairs={{0,8},{8,16},{16,24},{1,9},{9,17},{17,25},{2,10},{10,18},{18,26},{... | collective-permute-start | bytes 2359304 | tf_op jit(solution)/shard_map/ppermute | solution.py:213
  166.5 10.8 %collective-permute-done.2.refs_2_ = bf16[32,96,128]{2,1,0:T(8,128)(2,1)S(1)} collective-permute-done((bf16[32,96,128]{2,1,0:T(8,128)(2,1)S(1)}, bf16[32,96,128]{2,1,0:T(8,128)(2,1)S(1)}, u32[]{:S(2)}, u32[]{:S(2)}) %collective-permute-start.2) | collective-permute-done | bytes 786464 | tf_op jit(solution)/shard_map/ppermute | solution.py:213
  177.3 4.1 %collective-permute-done.1.refs_1_ = bf16[32,96,128]{2,1,0:T(8,128)(2,1)S(1)} collective-permute-done((bf16[32,96,128]{2,1,0:T(8,128)(2,1)S(1)}, bf16[32,96,128]{2,1,0:T(8,128)(2,1)S(1)}, u32[]{:S(2)}, u32[]{:S(2)}) %collective-permute-start.1) | collective-permute-done | bytes 786464 | tf_op jit(solution)/shard_map/ppermute | solution.py:213
  181.3 11.8 %collective-permute-done.23.refs_20_ = bf16[32,96,128]{2,1,0:T(8,128)(2,1)S(1)} collective-permute-done((bf16[32,96,128]{2,1,0:T(8,128)(2,1)S(1)}, bf16[32,96,128]{2,1,0:T(8,128)(2,1)S(1)}, u32[]{:S(2)}, u32[]{:S(2)}) %collective-permute-start.23) | collective-permute-done | bytes 786464 | tf_op jit(solution)/shard_map/ppermute | solution.py:213
  194.0 3.2 collective-permute-done.22.refs_19_
  197.2 131.2 %shard_map.50 = (bf16[5,32,48,128]{3,2,1,0:T(8,128)(2,1)}, bf16[15,32,48,128]{3,2,1,0:T(8,128)(2,1)}) custom-call(s32[20]{0:T(128)} %constant.43.clone.first_table, s32[20]{0:T(128)} %constant.44.clone.second_table, f32[32]{0:T(128)} %broadcast_divide_fusion.scale_x_ref, bf16[2,256,128]{2,1,0:T(8,128)(2,1)} %pad_maximum_fusion.15.wz_ref, ...), custom_call_target="tpu_custom_call" | custom-call | tf_op jit(solution)/shard_map/pallas_call | solution.py:265
  (187 shorter events, 52.8 us)
Async XLA Ops:
  2.4 40.8 %collective-permute-start.28 = (bf16[32,48,128]{2,1,0:T(8,128)(2,1)S(1)}, bf16[32,48,128]{2,1,0:T(8,128)(2,1)S(1)}, u32[]{:S(2)}, u32[]{:S(2)}) collective-permute-start(bf16[32,48,128]{2,1,0:T(8,128)(2,1)S(1)} %get-tuple-element.2), channel_id=1, source_target_pairs={{0,4},{4,0},{1,5},{5,1},{2,6},{6,2},{3,7},{7,3},{8,12},{12,8},{9,1... | collective-permute-start | bytes 1179656 | tf_op jit(solution)/shard_map/ppermute | solution.py:213
  4.5 48.0 %collective-permute-start.14 = (bf16[32,48,128]{2,1,0:T(8,128)(2,1)S(1)}, bf16[32,48,128]{2,1,0:T(8,128)(2,1)S(1)}, u32[]{:S(2)}, u32[]{:S(2)}) collective-permute-start(bf16[32,48,128]{2,1,0:T(8,128)(2,1)S(1)} %get-tuple-element.3), channel_id=1, source_target_pairs={{0,4},{4,0},{1,5},{5,1},{2,6},{6,2},{3,7},{7,3},{8,12},{12,8},{9,1... | collective-permute-start | bytes 1179656 | tf_op jit(solution)/shard_map/ppermute | solution.py:213
  4.6 43.9 %collective-permute-start.7 = (bf16[32,48,128]{2,1,0:T(8,128)(2,1)S(1)}, bf16[32,48,128]{2,1,0:T(8,128)(2,1)}, u32[]{:S(2)}, u32[]{:S(2)}) collective-permute-start(bf16[32,48,128]{2,1,0:T(8,128)(2,1)S(1)} %get-tuple-element.4), channel_id=1, source_target_pairs={{0,4},{4,0},{1,5},{5,1},{2,6},{6,2},{3,7},{7,3},{8,12},{12,8},{9,1... | collective-permute-start | bytes 1179656 | tf_op jit(solution)/shard_map/ppermute | solution.py:213
  6.0 32.6 %collective-permute-start = (bf16[32,48,128]{2,1,0:T(8,128)(2,1)S(1)}, bf16[32,48,128]{2,1,0:T(8,128)(2,1)S(1)}, u32[]{:S(2)}, u32[]{:S(2)}) collective-permute-start(bf16[32,48,128]{2,1,0:T(8,128)(2,1)S(1)} %get-tuple-element.5), channel_id=1, source_target_pairs={{0,4},{4,0},{1,5},{5,1},{2,6},{6,2},{3,7},{7,3},{8,12},{12,8},{9,1... | collective-permute-start | bytes 1179656 | tf_op jit(solution)/shard_map/ppermute | solution.py:213
  6.1 41.0 %collective-permute-start.21 = (bf16[32,48,128]{2,1,0:T(8,128)(2,1)S(1)}, bf16[32,48,128]{2,1,0:T(8,128)(2,1)S(1)}, u32[]{:S(2)}, u32[]{:S(2)}) collective-permute-start(bf16[32,48,128]{2,1,0:T(8,128)(2,1)S(1)} %get-tuple-element.6), channel_id=1, source_target_pairs={{0,4},{4,0},{1,5},{5,1},{2,6},{6,2},{3,7},{7,3},{8,12},{12,8},{9,1... | collective-permute-start | bytes 1179656 | tf_op jit(solution)/shard_map/ppermute | solution.py:213
  54.1 23.2 %collective-permute-start.18 = (bf16[32,24,128]{2,1,0:T(8,128)(2,1)S(1)}, bf16[32,24,128]{2,1,0:T(8,128)(2,1)S(1)}, u32[]{:S(2)}, u32[]{:S(2)}) collective-permute-start(bf16[32,24,128]{2,1,0:T(8,128)(2,1)S(1)} %pad_maximum_fusion.10), channel_id=1, source_target_pairs={{0,3},{1,0},{2,1},{3,2},{4,7},{5,4},{6,5},{7,6},{8,11},{9,8},{10,9... | collective-permute-start | bytes 589832 | tf_op jit(solution)/shard_map/ppermute | solution.py:213
  60.9 19.2 %collective-permute-start.6 = (bf16[32,48,128]{2,1,0:T(8,128)(2,1)S(1)}, bf16[32,48,128]{2,1,0:T(8,128)(2,1)S(1)}, u32[]{:S(2)}, u32[]{:S(2)}) collective-permute-start(bf16[32,48,128]{2,1,0:T(8,128)(2,1)S(1)} %maximum_maximum_fusion.refs_3_), channel_id=1, source_target_pairs={{8,0},{16,8},{24,16},{9,1},{17,9},{25,17},{10,2},{18,10},{26,18},{... | collective-permute-start | bytes 1179656 | tf_op jit(solution)/shard_map/ppermute | solution.py:213
  68.1 16.1 %collective-permute-start.5 = (bf16[32,48,128]{2,1,0:T(8,128)(2,1)S(1)}, bf16[32,48,128]{2,1,0:T(8,128)(2,1)S(1)}, u32[]{:S(2)}, u32[]{:S(2)}) collective-permute-start(bf16[32,48,128]{2,1,0:T(8,128)(2,1)S(1)} %maximum_maximum_fusion.refs_3_), channel_id=1, source_target_pairs={{0,8},{8,16},{16,24},{1,9},{9,17},{17,25},{2,10},{10,18},{18,26},{... | collective-permute-start | bytes 1179656 | tf_op jit(solution)/shard_map/ppermute | solution.py:213
  73.1 16.4 %collective-permute-start.26 = (bf16[32,48,128]{2,1,0:T(8,128)(2,1)S(1)}, bf16[32,48,128]{2,1,0:T(8,128)(2,1)S(1)}, u32[]{:S(2)}, u32[]{:S(2)}) collective-permute-start(bf16[32,48,128]{2,1,0:T(8,128)(2,1)S(1)} %maximum_maximum_fusion.3.refs_21_), channel_id=1, source_target_pairs={{0,8},{8,16},{16,24},{1,9},{9,17},{17,25},{2,10},{10,18},{18,26},{... | collective-permute-start | bytes 1179656 | tf_op jit(solution)/shard_map/ppermute | solution.py:213
  80.1 18.1 %collective-permute-start.33 = (bf16[32,48,128]{2,1,0:T(8,128)(2,1)S(1)}, bf16[32,48,128]{2,1,0:T(8,128)(2,1)S(1)}, u32[]{:S(2)}, u32[]{:S(2)}) collective-permute-start(bf16[32,48,128]{2,1,0:T(8,128)(2,1)S(1)} %maximum_maximum_fusion.4.refs_27_), channel_id=1, source_target_pairs={{0,8},{8,16},{16,24},{1,9},{9,17},{17,25},{2,10},{10,18},{18,26},{... | collective-permute-start | bytes 1179656 | tf_op jit(solution)/shard_map/ppermute | solution.py:213
  84.2 17.2 %collective-permute-start.13 = (bf16[32,48,128]{2,1,0:T(8,128)(2,1)S(1)}, bf16[32,48,128]{2,1,0:T(8,128)(2,1)S(1)}, u32[]{:S(2)}, u32[]{:S(2)}) collective-permute-start(bf16[32,48,128]{2,1,0:T(8,128)(2,1)S(1)} %maximum_maximum_fusion.1.refs_9_), channel_id=1, source_target_pairs={{8,0},{16,8},{24,16},{9,1},{17,9},{25,17},{10,2},{18,10},{26,18},{... | collective-permute-start | bytes 1179656 | tf_op jit(solution)/shard_map/ppermute | solution.py:213
  85.5 20.0 %collective-permute-start.12 = (bf16[32,48,128]{2,1,0:T(8,128)(2,1)S(1)}, bf16[32,48,128]{2,1,0:T(8,128)(2,1)S(1)}, u32[]{:S(2)}, u32[]{:S(2)}) collective-permute-start(bf16[32,48,128]{2,1,0:T(8,128)(2,1)S(1)} %maximum_maximum_fusion.1.refs_9_), channel_id=1, source_target_pairs={{0,8},{8,16},{16,24},{1,9},{9,17},{17,25},{2,10},{10,18},{18,26},{... | collective-permute-start | bytes 1179656 | tf_op jit(solution)/shard_map/ppermute | solution.py:213
  89.5 20.3 %collective-permute-start.20 = (bf16[32,48,128]{2,1,0:T(8,128)(2,1)S(1)}, bf16[32,48,128]{2,1,0:T(8,128)(2,1)S(1)}, u32[]{:S(2)}, u32[]{:S(2)}) collective-permute-start(bf16[32,48,128]{2,1,0:T(8,128)(2,1)S(1)} %maximum_maximum_fusion.2.refs_15_), channel_id=1, source_target_pairs={{8,0},{16,8},{24,16},{9,1},{17,9},{25,17},{10,2},{18,10},{26,18},{... | collective-permute-start | bytes 1179656 | tf_op jit(solution)/shard_map/ppermute | solution.py:213
  93.0 20.9 %collective-permute-start.19 = (bf16[32,48,128]{2,1,0:T(8,128)(2,1)S(1)}, bf16[32,48,128]{2,1,0:T(8,128)(2,1)}, u32[]{:S(2)}, u32[]{:S(2)}) collective-permute-start(bf16[32,48,128]{2,1,0:T(8,128)(2,1)S(1)} %maximum_maximum_fusion.2.refs_15_), channel_id=1, source_target_pairs={{0,8},{8,16},{16,24},{1,9},{9,17},{17,25},{2,10},{10,18},{18,26},{... | collective-permute-start | bytes 1179656 | tf_op jit(solution)/shard_map/ppermute | solution.py:213
  98.2 28.5 %collective-permute-start.30 = (bf16[32,96,128]{2,1,0:T(8,128)(2,1)S(1)}, bf16[32,96,128]{2,1,0:T(8,128)(2,1)S(1)}, u32[]{:S(2)}, u32[]{:S(2)}) collective-permute-start(bf16[32,96,128]{2,1,0:T(8,128)(2,1)S(1)} %pad_maximum_fusion.4.refs_24_), channel_id=1, source_target_pairs={{8,0},{16,8},{24,16},{9,1},{17,9},{25,17},{10,2},{18,10},{26,18},{... | collective-permute-start | bytes 2359304 | tf_op jit(solution)/shard_map/ppermute | solution.py:213
  101.4 29.3 %collective-permute-start.29 = (bf16[32,96,128]{2,1,0:T(8,128)(2,1)S(1)}, bf16[32,96,128]{2,1,0:T(8,128)(2,1)S(1)}, u32[]{:S(2)}, u32[]{:S(2)}) collective-permute-start(bf16[32,96,128]{2,1,0:T(8,128)(2,1)S(1)} %pad_maximum_fusion.4.refs_24_), channel_id=1, source_target_pairs={{0,8},{8,16},{16,24},{1,9},{9,17},{17,25},{2,10},{10,18},{18,26},{... | collective-permute-start | bytes 2359304 | tf_op jit(solution)/shard_map/ppermute | solution.py:213
  105.5 38.1 %collective-permute-start.16 = (bf16[32,96,128]{2,1,0:T(8,128)(2,1)S(1)}, bf16[32,96,128]{2,1,0:T(8,128)(2,1)S(1)}, u32[]{:S(2)}, u32[]{:S(2)}) collective-permute-start(bf16[32,96,128]{2,1,0:T(8,128)(2,1)S(1)} %pad_maximum_fusion.2.refs_12_), channel_id=1, source_target_pairs={{8,0},{16,8},{24,16},{9,1},{17,9},{25,17},{10,2},{18,10},{26,18},{... | collective-permute-start | bytes 2359304 | tf_op jit(solution)/shard_map/ppermute | solution.py:213
  109.9 37.8 %collective-permute-start.15 = (bf16[32,96,128]{2,1,0:T(8,128)(2,1)S(1)}, bf16[32,96,128]{2,1,0:T(8,128)(2,1)S(1)}, u32[]{:S(2)}, u32[]{:S(2)}) collective-permute-start(bf16[32,96,128]{2,1,0:T(8,128)(2,1)S(1)} %pad_maximum_fusion.2.refs_12_), channel_id=1, source_target_pairs={{0,8},{8,16},{16,24},{1,9},{9,17},{17,25},{2,10},{10,18},{18,26},{... | collective-permute-start | bytes 2359304 | tf_op jit(solution)/shard_map/ppermute | solution.py:213
  113.9 46.5 %collective-permute-start.9 = (bf16[32,96,128]{2,1,0:T(8,128)(2,1)S(1)}, bf16[32,96,128]{2,1,0:T(8,128)(2,1)S(1)}, u32[]{:S(2)}, u32[]{:S(2)}) collective-permute-start(bf16[32,96,128]{2,1,0:T(8,128)(2,1)S(1)} %pad_maximum_fusion.1.refs_6_), channel_id=1, source_target_pairs={{8,0},{16,8},{24,16},{9,1},{17,9},{25,17},{10,2},{18,10},{26,18},{... | collective-permute-start | bytes 2359304 | tf_op jit(solution)/shard_map/ppermute | solution.py:213
  126.7 39.8 %collective-permute-start.8 = (bf16[32,96,128]{2,1,0:T(8,128)(2,1)S(1)}, bf16[32,96,128]{2,1,0:T(8,128)(2,1)S(1)}, u32[]{:S(2)}, u32[]{:S(2)}) collective-permute-start(bf16[32,96,128]{2,1,0:T(8,128)(2,1)S(1)} %pad_maximum_fusion.1.refs_6_), channel_id=1, source_target_pairs={{0,8},{8,16},{16,24},{1,9},{9,17},{17,25},{2,10},{10,18},{18,26},{... | collective-permute-start | bytes 2359304 | tf_op jit(solution)/shard_map/ppermute | solution.py:213
  130.8 46.5 %collective-permute-start.2 = (bf16[32,96,128]{2,1,0:T(8,128)(2,1)S(1)}, bf16[32,96,128]{2,1,0:T(8,128)(2,1)S(1)}, u32[]{:S(2)}, u32[]{:S(2)}) collective-permute-start(bf16[32,96,128]{2,1,0:T(8,128)(2,1)S(1)} %pad_maximum_fusion.refs_0_), channel_id=1, source_target_pairs={{8,0},{16,8},{24,16},{9,1},{17,9},{25,17},{10,2},{18,10},{26,18},{... | collective-permute-start | bytes 2359304 | tf_op jit(solution)/shard_map/ppermute | solution.py:213
  143.6 37.8 %collective-permute-start.1 = (bf16[32,96,128]{2,1,0:T(8,128)(2,1)S(1)}, bf16[32,96,128]{2,1,0:T(8,128)(2,1)S(1)}, u32[]{:S(2)}, u32[]{:S(2)}) collective-permute-start(bf16[32,96,128]{2,1,0:T(8,128)(2,1)S(1)} %pad_maximum_fusion.refs_0_), channel_id=1, source_target_pairs={{0,8},{8,16},{16,24},{1,9},{9,17},{17,25},{2,10},{10,18},{18,26},{... | collective-permute-start | bytes 2359304 | tf_op jit(solution)/shard_map/ppermute | solution.py:213
  147.6 45.5 %collective-permute-start.23 = (bf16[32,96,128]{2,1,0:T(8,128)(2,1)S(1)}, bf16[32,96,128]{2,1,0:T(8,128)(2,1)S(1)}, u32[]{:S(2)}, u32[]{:S(2)}) collective-permute-start(bf16[32,96,128]{2,1,0:T(8,128)(2,1)S(1)} %pad_maximum_fusion.3.refs_18_), channel_id=1, source_target_pairs={{8,0},{16,8},{24,16},{9,1},{17,9},{25,17},{10,2},{18,10},{26,18},{... | collective-permute-start | bytes 2359304 | tf_op jit(solution)/shard_map/ppermute | solution.py:213
  160.4 36.7 %collective-permute-start.22 = (bf16[32,96,128]{2,1,0:T(8,128)(2,1)S(1)}, bf16[32,96,128]{2,1,0:T(8,128)(2,1)}, u32[]{:S(2)}, u32[]{:S(2)}) collective-permute-start(bf16[32,96,128]{2,1,0:T(8,128)(2,1)S(1)} %pad_maximum_fusion.3.refs_18_), channel_id=1, source_target_pairs={{0,8},{8,16},{16,24},{1,9},{9,17},{17,25},{2,10},{10,18},{18,26},{... | collective-permute-start | bytes 2359304 | tf_op jit(solution)/shard_map/ppermute | solution.py:213
  (54 other events, 1048.1 us)
where the time goes:
time: 330 us; the launch traced here: 329 us
  Pallas kernels  131 us (40%)
  waiting for transfers between devices  110 us (33%)
  starting transfers between devices  62.7 us (19%)
  local copies, waits for them, and re-layouts  14.2 us (4%)
  other arithmetic  8.62 us (3%)
    pallas_call x1, Pallas kernels, compact(): pl.pallas_call(functools.partial(filter_kernel, (depth_x, half, depth_z))...  131 us
    ppermute x35, waiting for transfers between devices, shift(): return lax.ppermute(block, axis, hops)  110 us
    ppermute x35, starting transfers between devices, shift(): return lax.ppermute(block, axis, hops)  62.7 us
  transfers between devices with their start and end apart: 35, of which 18 were waited for; matrix products, arithmetic and copies ran while one was open for 6% of the time, Pallas kernels for 0%

commit v1 on v0

--- a/solution.py
+++ b/solution.py
@@ -169,42 +169,48 @@
     pl.when(step < 5)(lambda: both(True))
     pl.when(step >= 5)(lambda: both(False))
 
-    def smooth(cell):
-        rim = narrow[cell, pl.ds(0, half), pl.ds(depth_z, 128)]
-        parts = []
-        for side in range(2):
-            mid = narrow[cell, pl.ds(side * half, half), pl.ds(0, depth_z)]
-            parts.append(
-                jnp.dot(
-                    jnp.concatenate([mid, rim], 1),
+    group = 8
+
+    def spans(plain):
+        def span(index, carry):
+            cells = pl.ds(index * group, group)
+            rim = narrow[cells, pl.ds(0, half), pl.ds(depth_z, 128)]
+            rim = rim.reshape(group * half, 128)
+            sides = []
+            for side in range(2):
+                mid = narrow[cells, pl.ds(side * half, half), pl.ds(0, depth_z)]
+                smooth = jnp.dot(
+                    jnp.concatenate([mid.reshape(group * half, depth_z), rim], 1),
                     wz_ref[side],
                     preferred_element_type=jnp.float32,
                 )
-            )
-        return (jnp.concatenate(parts, 0) * inverse).astype(jnp.bfloat16)
-
-    def pairs(index, carry):
-        for sub in range(2):
-            cell = 4 * index + 2 * sub
-            wide = jnp.concatenate([smooth(cell), smooth(cell + 1)], 1)
-            out = jnp.dot(wy_ref[...], wide, preferred_element_type=jnp.float32) * inverse
-            for k in range(2):
-                g = out[:, k * depth_z : (k + 1) * depth_z]
-
-                @pl.when(step < 5)
-                def _(k=k, g=g):
-                    means[step, cell + k] = g
-                    filtered_ref[0, cell + k] = g.astype(jnp.bfloat16)
-
-                @pl.when(step >= 5)
-                def _(k=k, g=g):
-                    stress_ref[0, cell + k] = (
-                        g - means[left, cell + k] * means[right, cell + k]
-                    ).astype(jnp.bfloat16)
-
-        return carry
-
-    lax.fori_loop(0, depth_x // 4, pairs, 0)
+                smooth = (smooth * inverse).astype(jnp.bfloat16)
+                sides.append(smooth.reshape(group, half, depth_z))
+            for pair in range(group // 2):
+                wide = jnp.concatenate(
+                    [
+                        jnp.concatenate([part[2 * pair + k] for part in sides], 0)
+                        for k in range(2)
+                    ],
+                    1,
+                )
+                out = jnp.dot(wy_ref[...], wide, preferred_element_type=jnp.float32) * inverse
+                for k in range(2):
+                    cell = index * group + 2 * pair + k
+                    g = out[:, k * depth_z : (k + 1) * depth_z]
+                    if plain:
+                        means[step, cell] = g
+                        filtered_ref[0, cell] = g.astype(jnp.bfloat16)
+                    else:
+                        stress_ref[0, cell] = (
+                            g - means[left, cell] * means[right, cell]
+                        ).astype(jnp.bfloat16)
+            return carry
+
+        lax.fori_loop(0, depth_x // group, span, 0)
+
+    pl.when(step < 5)(lambda: spans(True))
+    pl.when(step >= 5)(lambda: spans(False))
 
 
 def shift(block, axis, by, periodic):
@@ -296,7 +302,7 @@
             and half % 16 == 0
             and 2 * half >= 2 * R + 1
             and depth_x >= R
-            and depth_x % 4 == 0
+            and depth_x % 8 == 0
             and depth_z == 4 * R
         )
         return tuple(compact(fields)) if fits else body(fields)

time: 330 us -> 259 us (0.78)
  Pallas kernels: 131 us -> 60.8 us
    pallas_call x1, Pallas kernels: 131 us -> 60.8 us  [compact(): pl.pallas_call(functools.partial(filter_kernel, (depth_x, half, depth_z))...]
  transfers between devices with their start and end apart: 35 -> 35, of which waited for: 18 -> 18; matrix products, arithmetic and copies ran while one was open for 6% -> 8% of each run, Pallas kernels for 0% -> 0%
where the time goes in v1:
time: 259 us; the launch traced here: 258 us
  waiting for transfers between devices  110 us (42%)
  starting transfers between devices  62.7 us (24%)
  Pallas kernels  60.8 us (23%)
  local copies, waits for them, and re-layouts  14.2 us (5%)
  other arithmetic  8.62 us (3%)
    ppermute x35, waiting for transfers between devices, shift(): return lax.ppermute(block, axis, hops)  110 us
    ppermute x35, starting transfers between devices, shift(): return lax.ppermute(block, axis, hops)  62.7 us
    pallas_call x1, Pallas kernels, compact(): pl.pallas_call(functools.partial(filter_kernel, (depth_x, half, depth_z))...  60.8 us
    unnamed x92, local copies, waits for them, and re-layouts  5.33 us
  transfers between devices with their start and end apart: 35, of which 18 were waited for; matrix products, arithmetic and copies ran while one was open for 8% of the time, Pallas kernels for 0%

profile of v1, /device:TPU:1, one launch (start us, length us, event | category | flops | bytes accessed | tf_op | source)
XLA Modules:
  0.0 258.2 jit_solution(11810359372281450035)
XLA Ops:
  13.0 25.7 %collective-permute-done = bf16[32,48,128]{2,1,0:T(8,128)(2,1)S(1)} collective-permute-done((bf16[32,48,128]{2,1,0:T(8,128)(2,1)S(1)}, bf16[32,48,128]{2,1,0:T(8,128)(2,1)S(1)}, u32[]{:S(2)}, u32[]{:S(2)}) %collective-permute-start) | collective-permute-done | bytes 393248 | tf_op jit(solution)/shard_map/ppermute | solution.py:219
  39.1 3.8 %collective-permute-start.3 = (bf16[32,24,128]{2,1,0:T(8,128)(2,1)S(1)}, bf16[32,24,128]{2,1,0:T(8,128)(2,1)S(1)}, u32[]{:S(2)}, u32[]{:S(2)}) collective-permute-start(bf16[32,24,128]{2,1,0:T(8,128)(2,1)S(1)} %pad_maximum_fusion.5), channel_id=1, source_target_pairs={{0,1},{1,2},{2,3},{3,0},{4,5},{5,6},{6,7},{7,4},{8,9},{9,10},{10,1... | collective-permute-start | bytes 589832 | tf_op jit(solution)/shard_map/ppermute | solution.py:219
  44.3 2.8 %collective-permute-done.21 = bf16[32,48,128]{2,1,0:T(8,128)(2,1)S(1)} collective-permute-done((bf16[32,48,128]{2,1,0:T(8,128)(2,1)S(1)}, bf16[32,48,128]{2,1,0:T(8,128)(2,1)S(1)}, u32[]{:S(2)}, u32[]{:S(2)}) %collective-permute-start.21) | collective-permute-done | bytes 393248 | tf_op jit(solution)/shard_map/ppermute | solution.py:219
  55.3 4.1 %collective-permute-done.25 = bf16[32,24,128]{2,1,0:T(8,128)(2,1)S(1)} collective-permute-done((bf16[32,24,128]{2,1,0:T(8,128)(2,1)S(1)}, bf16[32,24,128]{2,1,0:T(8,128)(2,1)S(1)}, u32[]{:S(2)}, u32[]{:S(2)}) %collective-permute-start.25) | collective-permute-done | bytes 196640 | tf_op jit(solution)/shard_map/ppermute | solution.py:219
  63.5 4.6 %collective-permute-done.11 = bf16[32,24,128]{2,1,0:T(8,128)(2,1)S(1)} collective-permute-done((bf16[32,24,128]{2,1,0:T(8,128)(2,1)S(1)}, bf16[32,24,128]{2,1,0:T(8,128)(2,1)S(1)}, u32[]{:S(2)}, u32[]{:S(2)}) %collective-permute-start.11) | collective-permute-done | bytes 196640 | tf_op jit(solution)/shard_map/ppermute | solution.py:219
  68.1 3.2 %collective-permute-start.5 = (bf16[32,48,128]{2,1,0:T(8,128)(2,1)S(1)}, bf16[32,48,128]{2,1,0:T(8,128)(2,1)S(1)}, u32[]{:S(2)}, u32[]{:S(2)}) collective-permute-start(bf16[32,48,128]{2,1,0:T(8,128)(2,1)S(1)} %maximum_maximum_fusion.refs_3_), channel_id=1, source_target_pairs={{0,8},{8,16},{16,24},{1,9},{9,17},{17,25},{2,10},{10,18},{18,26},{... | collective-permute-start | bytes 1179656 | tf_op jit(solution)/shard_map/ppermute | solution.py:219
  73.1 4.0 %collective-permute-start.26 = (bf16[32,48,128]{2,1,0:T(8,128)(2,1)S(1)}, bf16[32,48,128]{2,1,0:T(8,128)(2,1)S(1)}, u32[]{:S(2)}, u32[]{:S(2)}) collective-permute-start(bf16[32,48,128]{2,1,0:T(8,128)(2,1)S(1)} %maximum_maximum_fusion.3.refs_21_), channel_id=1, source_target_pairs={{0,8},{8,16},{16,24},{1,9},{9,17},{17,25},{2,10},{10,18},{18,26},{... | collective-permute-start | bytes 1179656 | tf_op jit(solution)/shard_map/ppermute | solution.py:219
  80.1 4.0 %collective-permute-start.33 = (bf16[32,48,128]{2,1,0:T(8,128)(2,1)S(1)}, bf16[32,48,128]{2,1,0:T(8,128)(2,1)S(1)}, u32[]{:S(2)}, u32[]{:S(2)}) collective-permute-start(bf16[32,48,128]{2,1,0:T(8,128)(2,1)S(1)} %maximum_maximum_fusion.4.refs_27_), channel_id=1, source_target_pairs={{0,8},{8,16},{16,24},{1,9},{9,17},{17,25},{2,10},{10,18},{18,26},{... | collective-permute-start | bytes 1179656 | tf_op jit(solution)/shard_map/ppermute | solution.py:219
  85.5 4.0 %collective-permute-start.12 = (bf16[32,48,128]{2,1,0:T(8,128)(2,1)S(1)}, bf16[32,48,128]{2,1,0:T(8,128)(2,1)S(1)}, u32[]{:S(2)}, u32[]{:S(2)}) collective-permute-start(bf16[32,48,128]{2,1,0:T(8,128)(2,1)S(1)} %maximum_maximum_fusion.1.refs_9_), channel_id=1, source_target_pairs={{0,8},{8,16},{16,24},{1,9},{9,17},{17,25},{2,10},{10,18},{18,26},{... | collective-permute-start | bytes 1179656 | tf_op jit(solution)/shard_map/ppermute | solution.py:219
  93.0 3.9 %collective-permute-start.19 = (bf16[32,48,128]{2,1,0:T(8,128)(2,1)S(1)}, bf16[32,48,128]{2,1,0:T(8,128)(2,1)}, u32[]{:S(2)}, u32[]{:S(2)}) collective-permute-start(bf16[32,48,128]{2,1,0:T(8,128)(2,1)S(1)} %maximum_maximum_fusion.2.refs_15_), channel_id=1, source_target_pairs={{0,8},{8,16},{16,24},{1,9},{9,17},{17,25},{2,10},{10,18},{18,26},{... | collective-permute-start | bytes 1179656 | tf_op jit(solution)/shard_map/ppermute | solution.py:219
  101.4 3.2 %collective-permute-start.29 = (bf16[32,96,128]{2,1,0:T(8,128)(2,1)S(1)}, bf16[32,96,128]{2,1,0:T(8,128)(2,1)S(1)}, u32[]{:S(2)}, u32[]{:S(2)}) collective-permute-start(bf16[32,96,128]{2,1,0:T(8,128)(2,1)S(1)} %pad_maximum_fusion.4.refs_24_), channel_id=1, source_target_pairs={{0,8},{8,16},{16,24},{1,9},{9,17},{17,25},{2,10},{10,18},{18,26},{... | collective-permute-start | bytes 2359304 | tf_op jit(solution)/shard_map/ppermute | solution.py:219
  106.8 3.1 %collective-permute-done.20.refs_17_ = bf16[32,48,128]{2,1,0:T(8,128)(2,1)S(1)} collective-permute-done((bf16[32,48,128]{2,1,0:T(8,128)(2,1)S(1)}, bf16[32,48,128]{2,1,0:T(8,128)(2,1)S(1)}, u32[]{:S(2)}, u32[]{:S(2)}) %collective-permute-start.20) | collective-permute-done | bytes 393248 | tf_op jit(solution)/shard_map/ppermute | solution.py:219
  109.9 3.3 %collective-permute-start.15 = (bf16[32,96,128]{2,1,0:T(8,128)(2,1)S(1)}, bf16[32,96,128]{2,1,0:T(8,128)(2,1)S(1)}, u32[]{:S(2)}, u32[]{:S(2)}) collective-permute-start(bf16[32,96,128]{2,1,0:T(8,128)(2,1)S(1)} %pad_maximum_fusion.2.refs_12_), channel_id=1, source_target_pairs={{0,8},{8,16},{16,24},{1,9},{9,17},{17,25},{2,10},{10,18},{18,26},{... | collective-permute-start | bytes 2359304 | tf_op jit(solution)/shard_map/ppermute | solution.py:219
  116.8 9.9 %collective-permute-done.30.refs_26_ = bf16[32,96,128]{2,1,0:T(8,128)(2,1)S(1)} collective-permute-done((bf16[32,96,128]{2,1,0:T(8,128)(2,1)S(1)}, bf16[32,96,128]{2,1,0:T(8,128)(2,1)S(1)}, u32[]{:S(2)}, u32[]{:S(2)}) %collective-permute-start.30) | collective-permute-done | bytes 786464 | tf_op jit(solution)/shard_map/ppermute | solution.py:219
  126.7 3.2 %collective-permute-start.8 = (bf16[32,96,128]{2,1,0:T(8,128)(2,1)S(1)}, bf16[32,96,128]{2,1,0:T(8,128)(2,1)S(1)}, u32[]{:S(2)}, u32[]{:S(2)}) collective-permute-start(bf16[32,96,128]{2,1,0:T(8,128)(2,1)S(1)} %pad_maximum_fusion.1.refs_6_), channel_id=1, source_target_pairs={{0,8},{8,16},{16,24},{1,9},{9,17},{17,25},{2,10},{10,18},{18,26},{... | collective-permute-start | bytes 2359304 | tf_op jit(solution)/shard_map/ppermute | solution.py:219
  132.0 11.5 %collective-permute-done.16.refs_14_ = bf16[32,96,128]{2,1,0:T(8,128)(2,1)S(1)} collective-permute-done((bf16[32,96,128]{2,1,0:T(8,128)(2,1)S(1)}, bf16[32,96,128]{2,1,0:T(8,128)(2,1)S(1)}, u32[]{:S(2)}, u32[]{:S(2)}) %collective-permute-start.16) | collective-permute-done | bytes 786464 | tf_op jit(solution)/shard_map/ppermute | solution.py:219
  143.6 3.2 %collective-permute-start.1 = (bf16[32,96,128]{2,1,0:T(8,128)(2,1)S(1)}, bf16[32,96,128]{2,1,0:T(8,128)(2,1)S(1)}, u32[]{:S(2)}, u32[]{:S(2)}) collective-permute-start(bf16[32,96,128]{2,1,0:T(8,128)(2,1)S(1)} %pad_maximum_fusion.refs_0_), channel_id=1, source_target_pairs={{0,8},{8,16},{16,24},{1,9},{9,17},{17,25},{2,10},{10,18},{18,26},{... | collective-permute-start | bytes 2359304 | tf_op jit(solution)/shard_map/ppermute | solution.py:219
  148.9 11.5 %collective-permute-done.9.refs_8_ = bf16[32,96,128]{2,1,0:T(8,128)(2,1)S(1)} collective-permute-done((bf16[32,96,128]{2,1,0:T(8,128)(2,1)S(1)}, bf16[32,96,128]{2,1,0:T(8,128)(2,1)S(1)}, u32[]{:S(2)}, u32[]{:S(2)}) %collective-permute-start.9) | collective-permute-done | bytes 786464 | tf_op jit(solution)/shard_map/ppermute | solution.py:219
  160.4 4.1 %collective-permute-start.22 = (bf16[32,96,128]{2,1,0:T(8,128)(2,1)S(1)}, bf16[32,96,128]{2,1,0:T(8,128)(2,1)}, u32[]{:S(2)}, u32[]{:S(2)}) collective-permute-start(bf16[32,96,128]{2,1,0:T(8,128)(2,1)S(1)} %pad_maximum_fusion.3.refs_18_), channel_id=1, source_target_pairs={{0,8},{8,16},{16,24},{1,9},{9,17},{17,25},{2,10},{10,18},{18,26},{... | collective-permute-start | bytes 2359304 | tf_op jit(solution)/shard_map/ppermute | solution.py:219
  166.5 10.8 %collective-permute-done.2.refs_2_ = bf16[32,96,128]{2,1,0:T(8,128)(2,1)S(1)} collective-permute-done((bf16[32,96,128]{2,1,0:T(8,128)(2,1)S(1)}, bf16[32,96,128]{2,1,0:T(8,128)(2,1)S(1)}, u32[]{:S(2)}, u32[]{:S(2)}) %collective-permute-start.2) | collective-permute-done | bytes 786464 | tf_op jit(solution)/shard_map/ppermute | solution.py:219
  177.3 4.1 %collective-permute-done.1.refs_1_ = bf16[32,96,128]{2,1,0:T(8,128)(2,1)S(1)} collective-permute-done((bf16[32,96,128]{2,1,0:T(8,128)(2,1)S(1)}, bf16[32,96,128]{2,1,0:T(8,128)(2,1)S(1)}, u32[]{:S(2)}, u32[]{:S(2)}) %collective-permute-start.1) | collective-permute-done | bytes 786464 | tf_op jit(solution)/shard_map/ppermute | solution.py:219
  181.3 11.8 %collective-permute-done.23.refs_20_ = bf16[32,96,128]{2,1,0:T(8,128)(2,1)S(1)} collective-permute-done((bf16[32,96,128]{2,1,0:T(8,128)(2,1)S(1)}, bf16[32,96,128]{2,1,0:T(8,128)(2,1)S(1)}, u32[]{:S(2)}, u32[]{:S(2)}) %collective-permute-start.23) | collective-permute-done | bytes 786464 | tf_op jit(solution)/shard_map/ppermute | solution.py:219
  194.0 3.2 %collective-permute-done.22.refs_19_ = bf16[32,96,128]{2,1,0:T(8,128)(2,1)} collective-permute-done((bf16[32,96,128]{2,1,0:T(8,128)(2,1)S(1)}, bf16[32,96,128]{2,1,0:T(8,128)(2,1)}, u32[]{:S(2)}, u32[]{:S(2)}) %collective-permute-start.22) | collective-permute-done | bytes 786464 | tf_op jit(solution)/shard_map/ppermute | solution.py:219
  197.2 60.8 %shard_map.50 = (bf16[5,32,48,128]{3,2,1,0:T(8,128)(2,1)}, bf16[15,32,48,128]{3,2,1,0:T(8,128)(2,1)}) custom-call(s32[20]{0:T(128)} %constant.43.clone.first_table, s32[20]{0:T(128)} %constant.44.clone.second_table, f32[32]{0:T(128)} %broadcast_divide_fusion.scale_x_ref, bf16[2,256,128]{2,1,0:T(8,128)(2,1)} %pad_maximum_fusion.15.wz_ref, ...), custom_call_target="tpu_custom_call" | custom-call | tf_op jit(solution)/shard_map/pallas_call | solution.py:271
  (187 shorter events, 52.8 us)
Async XLA Ops:
  2.4 40.8 %collective-permute-start.28 = (bf16[32,48,128]{2,1,0:T(8,128)(2,1)S(1)}, bf16[32,48,128]{2,1,0:T(8,128)(2,1)S(1)}, u32[]{:S(2)}, u32[]{:S(2)}) collective-permute-start(bf16[32,48,128]{2,1,0:T(8,128)(2,1)S(1)} %get-tuple-element.2), channel_id=1, source_target_pairs={{0,4},{4,0},{1,5},{5,1},{2,6},{6,2},{3,7},{7,3},{8,12},{12,8},{9,1... | collective-permute-start | bytes 1179656 | tf_op jit(solution)/shard_map/ppermute | solution.py:219
  4.5 48.0 %collective-permute-start.14 = (bf16[32,48,128]{2,1,0:T(8,128)(2,1)S(1)}, bf16[32,48,128]{2,1,0:T(8,128)(2,1)S(1)}, u32[]{:S(2)}, u32[]{:S(2)}) collective-permute-start(bf16[32,48,128]{2,1,0:T(8,128)(2,1)S(1)} %get-tuple-element.3), channel_id=1, source_target_pairs={{0,4},{4,0},{1,5},{5,1},{2,6},{6,2},{3,7},{7,3},{8,12},{12,8},{9,1... | collective-permute-start | bytes 1179656 | tf_op jit(solution)/shard_map/ppermute | solution.py:219
  4.6 43.9 %collective-permute-start.7 = (bf16[32,48,128]{2,1,0:T(8,128)(2,1)S(1)}, bf16[32,48,128]{2,1,0:T(8,128)(2,1)}, u32[]{:S(2)}, u32[]{:S(2)}) collective-permute-start(bf16[32,48,128]{2,1,0:T(8,128)(2,1)S(1)} %get-tuple-element.4), channel_id=1, source_target_pairs={{0,4},{4,0},{1,5},{5,1},{2,6},{6,2},{3,7},{7,3},{8,12},{12,8},{9,1... | collective-permute-start | bytes 1179656 | tf_op jit(solution)/shard_map/ppermute | solution.py:219
  6.0 32.6 %collective-permute-start = (bf16[32,48,128]{2,1,0:T(8,128)(2,1)S(1)}, bf16[32,48,128]{2,1,0:T(8,128)(2,1)S(1)}, u32[]{:S(2)}, u32[]{:S(2)}) collective-permute-start(bf16[32,48,128]{2,1,0:T(8,128)(2,1)S(1)} %get-tuple-element.5), channel_id=1, source_target_pairs={{0,4},{4,0},{1,5},{5,1},{2,6},{6,2},{3,7},{7,3},{8,12},{12,8},{9,1... | collective-permute-start | bytes 1179656 | tf_op jit(solution)/shard_map/ppermute | solution.py:219
  6.1 41.0 %collective-permute-start.21 = (bf16[32,48,128]{2,1,0:T(8,128)(2,1)S(1)}, bf16[32,48,128]{2,1,0:T(8,128)(2,1)S(1)}, u32[]{:S(2)}, u32[]{:S(2)}) collective-permute-start(bf16[32,48,128]{2,1,0:T(8,128)(2,1)S(1)} %get-tuple-element.6), channel_id=1, source_target_pairs={{0,4},{4,0},{1,5},{5,1},{2,6},{6,2},{3,7},{7,3},{8,12},{12,8},{9,1... | collective-permute-start | bytes 1179656 | tf_op jit(solution)/shard_map/ppermute | solution.py:219
  54.1 23.2 %collective-permute-start.18 = (bf16[32,24,128]{2,1,0:T(8,128)(2,1)S(1)}, bf16[32,24,128]{2,1,0:T(8,128)(2,1)S(1)}, u32[]{:S(2)}, u32[]{:S(2)}) collective-permute-start(bf16[32,24,128]{2,1,0:T(8,128)(2,1)S(1)} %pad_maximum_fusion.10), channel_id=1, source_target_pairs={{0,3},{1,0},{2,1},{3,2},{4,7},{5,4},{6,5},{7,6},{8,11},{9,8},{10,9... | collective-permute-start | bytes 589832 | tf_op jit(solution)/shard_map/ppermute | solution.py:219
  60.9 19.2 %collective-permute-start.6 = (bf16[32,48,128]{2,1,0:T(8,128)(2,1)S(1)}, bf16[32,48,128]{2,1,0:T(8,128)(2,1)S(1)}, u32[]{:S(2)}, u32[]{:S(2)}) collective-permute-start(bf16[32,48,128]{2,1,0:T(8,128)(2,1)S(1)} %maximum_maximum_fusion.refs_3_), channel_id=1, source_target_pairs={{8,0},{16,8},{24,16},{9,1},{17,9},{25,17},{10,2},{18,10},{26,18},{... | collective-permute-start | bytes 1179656 | tf_op jit(solution)/shard_map/ppermute | solution.py:219
  68.1 16.1 %collective-permute-start.5 = (bf16[32,48,128]{2,1,0:T(8,128)(2,1)S(1)}, bf16[32,48,128]{2,1,0:T(8,128)(2,1)S(1)}, u32[]{:S(2)}, u32[]{:S(2)}) collective-permute-start(bf16[32,48,128]{2,1,0:T(8,128)(2,1)S(1)} %maximum_maximum_fusion.refs_3_), channel_id=1, source_target_pairs={{0,8},{8,16},{16,24},{1,9},{9,17},{17,25},{2,10},{10,18},{18,26},{... | collective-permute-start | bytes 1179656 | tf_op jit(solution)/shard_map/ppermute | solution.py:219
  73.1 16.4 %collective-permute-start.26 = (bf16[32,48,128]{2,1,0:T(8,128)(2,1)S(1)}, bf16[32,48,128]{2,1,0:T(8,128)(2,1)S(1)}, u32[]{:S(2)}, u32[]{:S(2)}) collective-permute-start(bf16[32,48,128]{2,1,0:T(8,128)(2,1)S(1)} %maximum_maximum_fusion.3.refs_21_), channel_id=1, source_target_pairs={{0,8},{8,16},{16,24},{1,9},{9,17},{17,25},{2,10},{10,18},{18,26},{... | collective-permute-start | bytes 1179656 | tf_op jit(solution)/shard_map/ppermute | solution.py:219
  80.1 18.1 %collective-permute-start.33 = (bf16[32,48,128]{2,1,0:T(8,128)(2,1)S(1)}, bf16[32,48,128]{2,1,0:T(8,128)(2,1)S(1)}, u32[]{:S(2)}, u32[]{:S(2)}) collective-permute-start(bf16[32,48,128]{2,1,0:T(8,128)(2,1)S(1)} %maximum_maximum_fusion.4.refs_27_), channel_id=1, source_target_pairs={{0,8},{8,16},{16,24},{1,9},{9,17},{17,25},{2,10},{10,18},{18,26},{... | collective-permute-start | bytes 1179656 | tf_op jit(solution)/shard_map/ppermute | solution.py:219
  84.2 17.2 %collective-permute-start.13 = (bf16[32,48,128]{2,1,0:T(8,128)(2,1)S(1)}, bf16[32,48,128]{2,1,0:T(8,128)(2,1)S(1)}, u32[]{:S(2)}, u32[]{:S(2)}) collective-permute-start(bf16[32,48,128]{2,1,0:T(8,128)(2,1)S(1)} %maximum_maximum_fusion.1.refs_9_), channel_id=1, source_target_pairs={{8,0},{16,8},{24,16},{9,1},{17,9},{25,17},{10,2},{18,10},{26,18},{... | collective-permute-start | bytes 1179656 | tf_op jit(solution)/shard_map/ppermute | solution.py:219
  85.5 20.0 %collective-permute-start.12 = (bf16[32,48,128]{2,1,0:T(8,128)(2,1)S(1)}, bf16[32,48,128]{2,1,0:T(8,128)(2,1)S(1)}, u32[]{:S(2)}, u32[]{:S(2)}) collective-permute-start(bf16[32,48,128]{2,1,0:T(8,128)(2,1)S(1)} %maximum_maximum_fusion.1.refs_9_), channel_id=1, source_target_pairs={{0,8},{8,16},{16,24},{1,9},{9,17},{17,25},{2,10},{10,18},{18,26},{... | collective-permute-start | bytes 1179656 | tf_op jit(solution)/shard_map/ppermute | solution.py:219
  89.5 20.3 %collective-permute-start.20 = (bf16[32,48,128]{2,1,0:T(8,128)(2,1)S(1)}, bf16[32,48,128]{2,1,0:T(8,128)(2,1)S(1)}, u32[]{:S(2)}, u32[]{:S(2)}) collective-permute-start(bf16[32,48,128]{2,1,0:T(8,128)(2,1)S(1)} %maximum_maximum_fusion.2.refs_15_), channel_id=1, source_target_pairs={{8,0},{16,8},{24,16},{9,1},{17,9},{25,17},{10,2},{18,10},{26,18},{... | collective-permute-start | bytes 1179656 | tf_op jit(solution)/shard_map/ppermute | solution.py:219
  93.0 20.9 %collective-permute-start.19 = (bf16[32,48,128]{2,1,0:T(8,128)(2,1)S(1)}, bf16[32,48,128]{2,1,0:T(8,128)(2,1)}, u32[]{:S(2)}, u32[]{:S(2)}) collective-permute-start(bf16[32,48,128]{2,1,0:T(8,128)(2,1)S(1)} %maximum_maximum_fusion.2.refs_15_), channel_id=1, source_target_pairs={{0,8},{8,16},{16,24},{1,9},{9,17},{17,25},{2,10},{10,18},{18,26},{... | collective-permute-start | bytes 1179656 | tf_op jit(solution)/shard_map/ppermute | solution.py:219
  98.2 28.5 %collective-permute-start.30 = (bf16[32,96,128]{2,1,0:T(8,128)(2,1)S(1)}, bf16[32,96,128]{2,1,0:T(8,128)(2,1)S(1)}, u32[]{:S(2)}, u32[]{:S(2)}) collective-permute-start(bf16[32,96,128]{2,1,0:T(8,128)(2,1)S(1)} %pad_maximum_fusion.4.refs_24_), channel_id=1, source_target_pairs={{8,0},{16,8},{24,16},{9,1},{17,9},{25,17},{10,2},{18,10},{26,18},{... | collective-permute-start | bytes 2359304 | tf_op jit(solution)/shard_map/ppermute | solution.py:219
  101.4 29.3 %collective-permute-start.29 = (bf16[32,96,128]{2,1,0:T(8,128)(2,1)S(1)}, bf16[32,96,128]{2,1,0:T(8,128)(2,1)S(1)}, u32[]{:S(2)}, u32[]{:S(2)}) collective-permute-start(bf16[32,96,128]{2,1,0:T(8,128)(2,1)S(1)} %pad_maximum_fusion.4.refs_24_), channel_id=1, source_target_pairs={{0,8},{8,16},{16,24},{1,9},{9,17},{17,25},{2,10},{10,18},{18,26},{... | collective-permute-start | bytes 2359304 | tf_op jit(solution)/shard_map/ppermute | solution.py:219
  105.5 38.1 %collective-permute-start.16 = (bf16[32,96,128]{2,1,0:T(8,128)(2,1)S(1)}, bf16[32,96,128]{2,1,0:T(8,128)(2,1)S(1)}, u32[]{:S(2)}, u32[]{:S(2)}) collective-permute-start(bf16[32,96,128]{2,1,0:T(8,128)(2,1)S(1)} %pad_maximum_fusion.2.refs_12_), channel_id=1, source_target_pairs={{8,0},{16,8},{24,16},{9,1},{17,9},{25,17},{10,2},{18,10},{26,18},{... | collective-permute-start | bytes 2359304 | tf_op jit(solution)/shard_map/ppermute | solution.py:219
  109.9 37.8 %collective-permute-start.15 = (bf16[32,96,128]{2,1,0:T(8,128)(2,1)S(1)}, bf16[32,96,128]{2,1,0:T(8,128)(2,1)S(1)}, u32[]{:S(2)}, u32[]{:S(2)}) collective-permute-start(bf16[32,96,128]{2,1,0:T(8,128)(2,1)S(1)} %pad_maximum_fusion.2.refs_12_), channel_id=1, source_target_pairs={{0,8},{8,16},{16,24},{1,9},{9,17},{17,25},{2,10},{10,18},{18,26},{... | collective-permute-start | bytes 2359304 | tf_op jit(solution)/shard_map/ppermute | solution.py:219
  113.9 46.5 %collective-permute-start.9 = (bf16[32,96,128]{2,1,0:T(8,128)(2,1)S(1)}, bf16[32,96,128]{2,1,0:T(8,128)(2,1)S(1)}, u32[]{:S(2)}, u32[]{:S(2)}) collective-permute-start(bf16[32,96,128]{2,1,0:T(8,128)(2,1)S(1)} %pad_maximum_fusion.1.refs_6_), channel_id=1, source_target_pairs={{8,0},{16,8},{24,16},{9,1},{17,9},{25,17},{10,2},{18,10},{26,18},{... | collective-permute-start | bytes 2359304 | tf_op jit(solution)/shard_map/ppermute | solution.py:219
  126.7 39.8 %collective-permute-start.8 = (bf16[32,96,128]{2,1,0:T(8,128)(2,1)S(1)}, bf16[32,96,128]{2,1,0:T(8,128)(2,1)S(1)}, u32[]{:S(2)}, u32[]{:S(2)}) collective-permute-start(bf16[32,96,128]{2,1,0:T(8,128)(2,1)S(1)} %pad_maximum_fusion.1.refs_6_), channel_id=1, source_target_pairs={{0,8},{8,16},{16,24},{1,9},{9,17},{17,25},{2,10},{10,18},{18,26},{... | collective-permute-start | bytes 2359304 | tf_op jit(solution)/shard_map/ppermute | solution.py:219
  130.8 46.5 %collective-permute-start.2 = (bf16[32,96,128]{2,1,0:T(8,128)(2,1)S(1)}, bf16[32,96,128]{2,1,0:T(8,128)(2,1)S(1)}, u32[]{:S(2)}, u32[]{:S(2)}) collective-permute-start(bf16[32,96,128]{2,1,0:T(8,128)(2,1)S(1)} %pad_maximum_fusion.refs_0_), channel_id=1, source_target_pairs={{8,0},{16,8},{24,16},{9,1},{17,9},{25,17},{10,2},{18,10},{26,18},{... | collective-permute-start | bytes 2359304 | tf_op jit(solution)/shard_map/ppermute | solution.py:219
  143.6 37.8 %collective-permute-start.1 = (bf16[32,96,128]{2,1,0:T(8,128)(2,1)S(1)}, bf16[32,96,128]{2,1,0:T(8,128)(2,1)S(1)}, u32[]{:S(2)}, u32[]{:S(2)}) collective-permute-start(bf16[32,96,128]{2,1,0:T(8,128)(2,1)S(1)} %pad_maximum_fusion.refs_0_), channel_id=1, source_target_pairs={{0,8},{8,16},{16,24},{1,9},{9,17},{17,25},{2,10},{10,18},{18,26},{... | collective-permute-start | bytes 2359304 | tf_op jit(solution)/shard_map/ppermute | solution.py:219
  147.6 45.5 %collective-permute-start.23 = (bf16[32,96,128]{2,1,0:T(8,128)(2,1)S(1)}, bf16[32,96,128]{2,1,0:T(8,128)(2,1)S(1)}, u32[]{:S(2)}, u32[]{:S(2)}) collective-permute-start(bf16[32,96,128]{2,1,0:T(8,128)(2,1)S(1)} %pad_maximum_fusion.3.refs_18_), channel_id=1, source_target_pairs={{8,0},{16,8},{24,16},{9,1},{17,9},{25,17},{10,2},{18,10},{26,18},{... | collective-permute-start | bytes 2359304 | tf_op jit(solution)/shard_map/ppermute | solution.py:219
  160.4 36.7 %collective-permute-start.22 = (bf16[32,96,128]{2,1,0:T(8,128)(2,1)S(1)}, bf16[32,96,128]{2,1,0:T(8,128)(2,1)}, u32[]{:S(2)}, u32[]{:S(2)}) collective-permute-start(bf16[32,96,128]{2,1,0:T(8,128)(2,1)S(1)} %pad_maximum_fusion.3.refs_18_), channel_id=1, source_target_pairs={{0,8},{8,16},{16,24},{1,9},{9,17},{17,25},{2,10},{10,18},{18,26},{... | collective-permute-start | bytes 2359304 | tf_op jit(solution)/shard_map/ppermute | solution.py:219
  (54 other events, 1048.1 us)
